TPU v7x, 256 devices: a whole 4x4x8 slice. The times are simulated.
256 devices in a mesh: seq: 64 (over z, y, core), hid: 4 (over x).
Axes of the slice: x: 4, y: 4, z: 8, core: 2. Of those that a mesh axis runs over, the one named last changes fastest.
Arguments:
- gate_half: bfloat16 [8192, 2048], P('seq', 'hid'), may hold values from -6 to 6
- value_half: bfloat16 [8192, 2048], P('seq', 'hid'), may hold values from -6 to 6
- norm_gain: float32 [2048], P('hid'), may hold values from 0.25 to 1.75
- norm_shift: float32 [2048], P('hid'), may hold values from -0.5 to 0.5
- token_weight: bfloat16 [8192, 8192], P('seq'), may hold values from -0.1875 to 0.1875
- token_bias: float32 [8192], P('seq'), may hold values from 0.5 to 1.5
- grad_output: bfloat16 [8192, 2048], P('seq', 'hid'), may hold values from -6 to 6
Outputs:
- grad_gate: bfloat16 [8192, 2048], P('seq', 'hid')
- grad_value: bfloat16 [8192, 2048], P('seq', 'hid')
- grad_gain: float32 [2048], P('hid')
- grad_shift: float32 [2048], P('hid')
- grad_weight: float32 [8192, 8192], P('seq', 'hid')
- grad_token_bias: float32 [8192], P('seq')
All inputs are finite; a program needn't handle non-finite values.
Results may differ from a plain program's by a relative error of at most 0.005.
Values may be sent and summed in bfloat16 or wider, within the bound.
A program may use at most 64 MiB of HBM per device.

v0:
```python
import jax
import jax.numpy as jnp
from jax import lax
from jax.sharding import PartitionSpec as P

HIDDEN_SIZE = 2048


def sent_to_all(array, axis):
    copies = jnp.broadcast_to(array, (lax.axis_size(axis), *array.shape))
    return lax.all_to_all(copies, axis, split_axis=0, concat_axis=0, tiled=True)


def taken_together(array, axis):
    everything = sent_to_all(array, axis)
    return jnp.sum(everything, axis=0)


def packed_total(arrays, axis):
    flat, at, gathered = (jnp.concatenate([a.reshape(-1) for a in arrays]), 0, [])
    subtotal = taken_together(flat, axis)
    for a in arrays:
        gathered.append(subtotal[at : at + a.size].reshape(a.shape))
        at += a.size
    return tuple(gathered)


def per_device(gate_half, value_half, norm_gain, norm_shift, token_weight, token_bias, grad_output):
    local_rows = gate_half.shape[0]
    channels = gate_half.shape[1]
    all_tokens = token_weight.shape[1]
    row_start = lax.axis_index("seq") * local_rows
    row_last = row_start + local_rows - 1
    row_ids = row_start + lax.iota(jnp.int32, local_rows)[:, None]
    second = value_half.astype(jnp.float32)
    upstream = grad_output.astype(jnp.float32)
    grad_mix = (upstream * gate_half.astype(jnp.float32)).astype(jnp.bfloat16)
    sum_first, sum_square, grad_token_bias = lax.psum(
        (
            jnp.sum(second, axis=1),
            jnp.sum(second * second, axis=1),
            jnp.sum(grad_mix.astype(jnp.float32), axis=1),
        ),
        "hid",
    )
    row_mean = (sum_first / HIDDEN_SIZE)[:, None]
    row_var = (sum_square / HIDDEN_SIZE)[:, None] - row_mean * row_mean
    inv_std = lax.rsqrt(row_var + 1e-05)
    centred = (second - row_mean) * inv_std
    normed = (centred * norm_gain + norm_shift).astype(jnp.bfloat16)
    start_pair = (
        jnp.zeros((local_rows, channels), jnp.float32),
        jnp.zeros((local_rows, all_tokens), jnp.float32),
    )
    shard_rows = lax.all_gather(normed, "seq", axis=0, tiled=True)
    length = shard_rows.shape[0]

    def compute(pair):
        weight_block = token_weight
        column_ids = lax.iota(jnp.int32, length)[None, :]
        lower_mask = column_ids <= row_ids
        weight_block = jnp.where(lower_mask, weight_block, jnp.zeros_like(weight_block))
        mixed_sum = jnp.dot(weight_block, shard_rows, preferred_element_type=jnp.float32)
        outer = jnp.einsum("tc,nc->tn", grad_mix, shard_rows, preferred_element_type=jnp.float32)
        outer = jnp.where(lower_mask, outer, 0.0)
        return (mixed_sum, outer)

    mixed_sum, weight_term = lax.cond(
        jnp.int32(0) <= row_last, compute, lambda pair: pair, start_pair
    )
    spatial = mixed_sum + token_bias[:, None]
    grad_gate = (upstream * spatial).astype(jnp.bfloat16)
    grad_weight = lax.psum_scatter(weight_term, "hid", scatter_dimension=1, tiled=True)
    columns = lax.all_to_all(token_weight, "seq", split_axis=1, concat_axis=0, tiled=True)
    own_ids = row_start + lax.iota(jnp.int32, local_rows)[None, :]
    fold_shard_rows = lax.all_gather(grad_mix, "seq", axis=0, tiled=True)
    fold_length = fold_shard_rows.shape[0]

    def compute(running):
        weight_block = columns
        source_ids = lax.iota(jnp.int32, fold_length)[:, None]
        weight_block = jnp.where(source_ids >= own_ids, weight_block, jnp.zeros_like(weight_block))
        return jnp.einsum(
            "nt,nc->tc", weight_block, fold_shard_rows, preferred_element_type=jnp.float32
        )

    grad_normed = lax.cond(
        jnp.int32(0) + fold_length - 1 >= row_start,
        compute,
        lambda running: running,
        jnp.zeros((local_rows, channels), jnp.float32),
    )
    grad_gain, grad_shift = packed_total(
        (jnp.sum(grad_normed * centred, axis=0), jnp.sum(grad_normed, axis=0)), "seq"
    )
    grad_centred = grad_normed * norm_gain
    sum_grad, sum_cross = lax.psum(
        (jnp.sum(grad_centred, axis=1), jnp.sum(grad_centred * centred, axis=1)), "hid"
    )
    first_mean = (sum_grad / HIDDEN_SIZE)[:, None]
    second_mean = (sum_cross / HIDDEN_SIZE)[:, None]
    grad_value = (inv_std * (grad_centred - first_mean - centred * second_mean)).astype(
        jnp.bfloat16
    )
    return (grad_gate, grad_value, grad_gain, grad_shift, grad_weight, grad_token_bias)


def solution(mesh):
    placed = (
        P("seq", "hid"),
        P("seq", "hid"),
        P("hid"),
        P("hid"),
        P("seq", None),
        P("seq"),
        P("seq", "hid"),
    )
    return jax.shard_map(
        per_device,
        mesh=mesh,
        in_specs=placed,
        out_specs=(P("seq", "hid"), P("seq", "hid"), P("hid"), P("hid"), P("seq", "hid"), P("seq")),
        check_vma=False,
    )
```

profile of v0, /device:TPU:1, one launch (start us, length us, event | category | flops | bytes accessed | tf_op | source)
XLA Modules:
  0.0 270.6 jit_solution(11396971279304036208)
XLA Ops:
  7.2 0.0 all-gather.5.cloned.1.call-start
  7.2 1.7 convert_reduce_fusion.1
  8.9 0.0 all-gather.5.cloned.1.call-update
  8.9 0.0 copy-start.3
  8.9 4.1 %copy.17 = bf16[128,8192]{0,1:T(8,128)(2,1)} copy(bf16[128,8192]{1,0:T(8,128)(2,1)} %param.15) | data formatting | bytes 4194304 | tf_op args[4]
  13.0 13.1 %all-to-all-start = ((bf16[128,64,128]{0,2,1:T(8,128)(2,1)}), bf16[128,64,128]{0,2,1:T(8,128)(2,1)S(1)}, u32[]{:S(2)}, u32[]{:S(2)}) async-start(bf16[128,64,128]{0,2,1:T(8,128)(2,1)} %bitcast.13), calls=%async_computation | async-start | bytes 4194304 | tf_op jit(solution)/shard_map/all_to_all | solution.py:74
  26.2 0.0 all-gather.3.cloned.1.call-start
  26.2 0.1 convert_reduce_fusion
  26.4 9.1 %all-reduce.1 = (f32[128]{0:T(128)S(1)}, f32[128]{0:T(128)S(1)}) all-reduce(f32[128]{0:T(128)S(1)} %get-tuple-element.62, f32[128]{0:T(128)S(1)} %get-tuple-element.61), channel_id=1, replica_groups=mesh['seq'=64,'hid'=4] {'hid'}, use_global_device_ids=true, to_apply=%region_3.0 | all-reduce | flops 256 | bytes 2048 | tf_op jit(solution)/shard_map/psum | solution.py:38
  35.5 48.1 %all-to-all-done = bf16[128,64,128]{0,2,1:T(8,128)(2,1)S(1)} async-done(((bf16[128,64,128]{0,2,1:T(8,128)(2,1)}), bf16[128,64,128]{0,2,1:T(8,128)(2,1)S(1)}, u32[]{:S(2)}, u32[]{:S(2)}) %all-to-all-start) | async-done | bytes 2097184 | tf_op jit(solution)/shard_map/all_to_all | solution.py:74
  83.6 23.1 %all-gather.5.cloned.1.call-done = bf16[8192,512]{1,0:T(8,128)(2,1)} async-done(((bf16[128,512]{1,0:T(8,128)(2,1)}), bf16[8192,512]{1,0:T(8,128)(2,1)}) %all-gather.5.cloned.1.call-update) | async-done | bytes 8388624 | tf_op jit(solution)/shard_map/all_gather | solution.py:76
  106.7 9.3 %conditional.3 = (f32[128,512]{1,0:T(8,128)S(1)}) conditional(s32[]{:T(128)} %convert_element_type.37, () %tuple.24, (s32[]{:T(128)}, s32[1,128]{1,0:T(1,128)S(1)}, bf16[64,128,128]{1,2,0:T(8,128)(2,1)S(1)}, bf16[8192,512]{1,0:T(8,128)(2,1)}) %tuple.49), branch_computations={%region_6.0_spmd, %region_7.8_spmd} | conditional | flops 1075839104 | bytes 23332392 | solution.py:87
  106.7 1.4 copy-done.1
  108.1 3.2 %copy.18 = bf16[64,128,128]{2,1,0:T(8,128)(2,1)S(1)} copy(bf16[64,128,128]{1,2,0:T(8,128)(2,1)} %copy-done.1) | data formatting | bytes 4194304 | tf_op jit(solution)/shard_map
  111.3 4.7 %fusion.7 = f32[128,512]{1,0:T(8,128)S(1)} fusion(bf16[8192,512]{1,0:T(8,128)(2,1)} %get-tuple-element.34, bf16[8192,128]{1,0:T(8,128)(2,1)S(1)} %bitcast.11, s32[128]{0:T(128)S(1)} %add_bitcast_fusion.1), kind=kOutput, calls=%fused_computation.10 | convolution fusion | flops 1075838976 | bytes 10748416 | tf_op jit(solution)/shard_map/cond/branch_1_fun/nt,nc->tc/dot_general | solution.py:83
  116.0 0.2 fusion.25
  116.2 9.0 %all-reduce = (f32[128]{0:T(128)S(1)}, f32[128]{0:T(128)S(1)}, f32[128]{0:T(128)}) all-reduce(f32[128]{0:T(128)S(1)} %get-tuple-element.58, f32[128]{0:T(128)S(1)} %get-tuple-element.59, f32[128]{0:T(128)S(1)} %get-tuple-element.68), channel_id=1, replica_groups=mesh['seq'=64,'hid'=4] {'hid'}, use_global_device_ids=true, to_apply=%region_11.12 | all-reduce | flops 384 | bytes 3072 | tf_op jit(solution)/shard_map/psum | solution.py:97
  125.2 0.9 fusion.24
  126.1 0.0 all-gather.3.cloned.1.call-update
  126.1 0.0 reduce-scatter.2.cloned.1.call-start
  126.2 80.8 %all-gather.3.cloned.1.call-done = bf16[8192,512]{1,0:T(8,128)(2,1)} async-done(((bf16[128,512]{1,0:T(8,128)(2,1)}), bf16[8192,512]{1,0:T(8,128)(2,1)}) %all-gather.3.cloned.1.call-update) | async-done | bytes 8388624 | tf_op jit(solution)/shard_map/all_gather | solution.py:55
  207.0 11.2 %conditional.2 = (f32[128,512]{1,0:T(8,128)S(1)}, f32[128,8192]{1,0:T(8,128)}) conditional(s32[]{:T(128)} %convert_element_type.31, () %tuple.22, (s32[]{:T(128)}, s32[128,1]{0,1:T(1,128)S(1)}, bf16[128,8192]{1,0:T(8,128)(2,1)}, bf16[8192,512]{1,0:T(8,128)(2,1)}, bf16[128,512]{1,0:T(8,128)(2,1)S(1)}) %tuple.50), branch_computations={%region_4.0_spmd, %region_5.0_spmd} | conditional | flops 2151677952 | bytes 57018416 | solution.py:68
  207.0 5.4 %fusion.1 = f32[128,512]{1,0:T(8,128)S(1)} fusion(bf16[8192,512]{1,0:T(8,128)(2,1)} %get-tuple-element.29, bf16[128,8192]{1,0:T(8,128)(2,1)} %get-tuple-element.28, s32[128]{0:T(128)S(1)} %add_bitcast_fusion), kind=kOutput, calls=%fused_computation.3 | convolution fusion | flops 1075838976 | bytes 10748416 | tf_op jit(solution)/shard_map/cond/branch_1_fun/dot_general | solution.py:63
  212.5 0.9 copy-done
  213.4 4.8 %convolution_select_fusion = f32[128,8192]{1,0:T(8,128)} fusion(bf16[128,512]{1,0:T(8,128)(2,1)S(1)} %get-tuple-element.30, bf16[8192,512]{1,0:T(8,128)(2,1)S(1)} %copy-done, s32[128]{0:T(128)S(1)} %add_bitcast_fusion), kind=kOutput, calls=%fused_computation | convolution fusion | flops 1075838976 | bytes 12714496 | tf_op jit(solution)/shard_map/cond/branch_1_fun/tc,nc->tn/dot_general | solution.py:64
  218.2 0.0 reduce-scatter.2.cloned.1.call-update
  218.2 0.1 broadcast_in_dim.8
  218.4 18.7 %all_to_all.25 = f32[64,1,1024]{2,1,0:T(1,128)S(1)} all-to-all(f32[64,1,1024]{2,1,0:T(1,128)S(1)} %broadcast_in_dim.8), channel_id=1, replica_groups=mesh['seq'=64,'hid'=4] {'seq'}, dimensions={0} | all-to-all | bytes 524288 | tf_op jit(solution)/shard_map/all_to_all | solution.py:11
  237.1 0.2 reduce_sum.78
  237.2 0.6 fusion.28
  237.8 0.8 fusion.13
  238.6 25.5 %reduce-scatter.2.cloned.1.call-done = f32[128,2048]{1,0:T(8,128)} async-done(((f32[128,8192]{1,0:T(8,128)}), f32[128,2048]{1,0:T(8,128)}) %reduce-scatter.2.cloned.1.call-update) | async-done | bytes 1048592 | tf_op jit(solution)/shard_map/reduce_scatter | solution.py:73
  (20 shorter events, 0.1 us)
Async XLA Ops:
  7.2 99.5 %all-gather.5.cloned.1.call-start = ((), (), s32[]{:S(2)}) async-start(), calls=%async_computation.4 | async-start | bytes 8519680 | tf_op jit(solution)/shard_map/all_gather | solution.py:76
  8.9 17.3 %copy-start.3 = (bf16[128,512]{1,0:T(8,128)(2,1)S(1)}, bf16[128,512]{1,0:T(8,128)(2,1)}, u32[]{:S(2)}) copy-start(bf16[128,512]{1,0:T(8,128)(2,1)} %param.12) | copy-start | bytes 393220
  13.0 70.6 %all-to-all-start = ((bf16[128,64,128]{0,2,1:T(8,128)(2,1)}), bf16[128,64,128]{0,2,1:T(8,128)(2,1)S(1)}, u32[]{:S(2)}, u32[]{:S(2)}) async-start(bf16[128,64,128]{0,2,1:T(8,128)(2,1)} %bitcast.13), calls=%async_computation | async-start | bytes 4194304 | tf_op jit(solution)/shard_map/all_to_all | solution.py:74
  26.2 180.8 %all-gather.3.cloned.1.call-start = ((), (), s32[]{:S(2)}) async-start(), calls=%async_computation.3 | async-start | bytes 8519680 | tf_op jit(solution)/shard_map/all_gather | solution.py:55
  106.7 9.3 %copy-start.5 = (f32[512]{0:T(512)S(1)}, f32[512]{0:T(512)}, u32[]{:S(2)}) copy-start(f32[512]{0:T(512)} %param.13) | copy-start | bytes 6148
  106.7 18.6 %copy-start.6 = (f32[512]{0:T(512)S(1)}, f32[512]{0:T(512)}, u32[]{:S(2)}) copy-start(f32[512]{0:T(512)} %param.14) | copy-start | bytes 6148
  106.7 100.3 %copy-start.2 = (bf16[128,512]{1,0:T(8,128)(2,1)S(1)}, bf16[128,512]{1,0:T(8,128)(2,1)}, u32[]{:S(2)}) copy-start(bf16[128,512]{1,0:T(8,128)(2,1)} %get-tuple-element.69) | copy-start | bytes 393220
  106.7 1.4 copy-start.1
  126.1 138.0 %reduce-scatter.2.cloned.1.call-start = ((), (), s32[]{:S(2)}) async-start(), calls=%async_computation.5 | async-start | bytes 5242880 | tf_op jit(solution)/shard_map/reduce_scatter | solution.py:73
  207.0 6.4 %copy-start = (bf16[8192,512]{1,0:T(8,128)(2,1)S(1)}, bf16[8192,512]{1,0:T(8,128)(2,1)}, u32[]{:S(2)}) copy-start(bf16[8192,512]{1,0:T(8,128)(2,1)} %get-tuple-element.29) | copy-start | bytes 25165828 | tf_op jit(solution)/shard_map/cond
  218.2 19.6 %copy-start.4 = (bf16[128,512]{1,0:T(8,128)(2,1)S(1)}, bf16[128,512]{1,0:T(8,128)(2,1)}, u32[]{:S(2)}) copy-start(bf16[128,512]{1,0:T(8,128)(2,1)} %param.17) | copy-start | bytes 393220
  218.2 19.6 %copy-start.7 = (f32[128]{0:T(128)S(1)}, f32[128]{0:T(128)}, u32[]{:S(2)}) copy-start(f32[128]{0:T(128)} %param.16) | copy-start | bytes 1540
Sparse Core Ops, SparseCore 0:
  11.3 95.2 all-gather.4
  126.2 80.7 all-gather.2
  218.4 45.6 reduce-scatter.1
where the time goes:
time: 271 us
  waiting for transfers between devices  178 us (66%)
  blocking collectives  36.8 us (14%)
  matrix products  15 us (6%)
  between operations  13.8 us (5%)
  starting transfers between devices  13.3 us (5%)
  local copies, waits for them, and re-layouts  10.4 us (4%)
  other arithmetic  3.82 us (1%)
    all_gather x1, waiting for transfers between devices, per_device(): shard_rows = lax.all_gather(normed, 'seq', axis=0, tiled=True)  80.8 us
    all_to_all x1, waiting for transfers between devices, per_device(): lax.all_to_all(token_weight, 'seq', split_axis=1, concat_axis=0, tiled=True)  48.1 us
    reduce_scatter x1, waiting for transfers between devices, per_device(): lax.psum_scatter(weight_term, 'hid', scatter_dimension=1, tiled=True)  25.5 us
    all_gather x1, waiting for transfers between devices, per_device(): fold_shard_rows = lax.all_gather(grad_mix, 'seq', axis=0, tiled=True)  23.1 us
    all_to_all x1, blocking collectives, sent_to_all(): return lax.all_to_all(copies, axis, split_axis=0, concat_axis=0, tiled=True)  18.7 us
    all_to_all x1, starting transfers between devices, per_device(): lax.all_to_all(token_weight, 'seq', split_axis=1, concat_axis=0, tiled=True)  13.1 us
    psum x1, blocking collectives, per_device(): lax.psum((jnp.sum(second, axis=1), jnp.sum(second * second, axis=1), jnp....  9.12 us
    psum x1, blocking collectives, per_device(): lax.psum((jnp.sum(grad_centred, axis=1), jnp.sum(grad_centred * centred,...  8.99 us
  transfers between devices with their start and end apart: 4, of which 4 were waited for; matrix products, arithmetic and copies ran while one was open for 2% of the time, Pallas kernels for 0%

commit v1 on v0

--- a/solution.py
+++ b/solution.py
@@ -52,7 +52,11 @@
         jnp.zeros((local_rows, channels), jnp.float32),
         jnp.zeros((local_rows, all_tokens), jnp.float32),
     )
-    shard_rows = lax.all_gather(normed, "seq", axis=0, tiled=True)
+    devices = lax.axis_size("seq")
+    repeats = [devices if d == 0 else 1 for d in range(normed.ndim)]
+    shard_rows = lax.all_to_all(
+        jnp.tile(normed, repeats), "seq", split_axis=0, concat_axis=0, tiled=True
+    )
     length = shard_rows.shape[0]
 
     def compute(pair):

time: 271 us -> 390 us (1.44)
  waiting for transfers between devices: 178 us -> 277 us
  starting transfers between devices: 13.3 us -> 22.4 us
  blocking collectives: 36.8 us -> 41.1 us
    all_to_all x0 -> x1, waiting for transfers between devices: none -> 182 us  [per_device(): lax.all_to_all(jnp.tile(normed, repeats), 'seq', split_axis=0, concat_axi...]
    all_gather x1 -> x0, waiting for transfers between devices: 80.8 us -> none  [per_device(): shard_rows = lax.all_gather(normed, 'seq', axis=0, tiled=True)]
    all_to_all x0 -> x1, starting transfers between devices: none -> 9.17 us  [per_device(): lax.all_to_all(jnp.tile(normed, repeats), 'seq', split_axis=0, concat_axi...]
    all_to_all x1, blocking collectives: 18.7 us -> 22.9 us  [sent_to_all(): return lax.all_to_all(copies, axis, split_axis=0, concat_axis=0, tiled=True)]
    another operation x1 -> x2, local copies, waits for them, and re-layouts: 3.22 us -> 7.44 us  [the longest x1 4.22 us: per_device(): jnp.tile(normed, repeats)]
where the time goes in v1:
time: 390 us
  waiting for transfers between devices  277 us (71%)
  blocking collectives  41.1 us (11%)
  starting transfers between devices  22.4 us (6%)
  matrix products  17.6 us (5%)
  between operations  14.1 us (4%)
  local copies, waits for them, and re-layouts  13.7 us (4%)
    all_to_all x1, waiting for transfers between devices, per_device(): lax.all_to_all(jnp.tile(normed, repeats), 'seq', split_axis=0, concat_axi...  182 us
    all_to_all x1, waiting for transfers between devices, per_device(): lax.all_to_all(token_weight, 'seq', split_axis=1, concat_axis=0, tiled=True)  47.9 us
    reduce_scatter x1, waiting for transfers between devices, per_device(): lax.psum_scatter(weight_term, 'hid', scatter_dimension=1, tiled=True)  23.4 us
    all_gather x1, waiting for transfers between devices, per_device(): fold_shard_rows = lax.all_gather(grad_mix, 'seq', axis=0, tiled=True)  23.3 us
    all_to_all x1, blocking collectives, sent_to_all(): return lax.all_to_all(copies, axis, split_axis=0, concat_axis=0, tiled=True)  22.9 us
    all_to_all x1, starting transfers between devices, per_device(): lax.all_to_all(token_weight, 'seq', split_axis=1, concat_axis=0, tiled=True)  13.1 us
    all_to_all x1, starting transfers between devices, per_device(): lax.all_to_all(jnp.tile(normed, repeats), 'seq', split_axis=0, concat_axi...  9.17 us
    psum x1, blocking collectives, per_device(): lax.psum((jnp.sum(second, axis=1), jnp.sum(second * second, axis=1), jnp....  9.17 us
  transfers between devices with their start and end apart: 4, of which 4 were waited for; matrix products, arithmetic and copies ran while one was open for 2% of the time, Pallas kernels for 0%

profile of v1, /device:TPU:1, one launch (start us, length us, event | category | flops | bytes accessed | tf_op | source)
XLA Modules:
  0.0 389.5 jit_solution(18036650060977032159)
XLA Ops:
  7.2 0.0 all-gather.2.cloned.1.call-start
  7.2 1.7 convert_reduce_fusion.1
  8.9 0.0 all-gather.2.cloned.1.call-update
  8.9 0.0 copy-start.3
  8.9 4.1 %copy.17 = bf16[128,8192]{0,1:T(8,128)(2,1)} copy(bf16[128,8192]{1,0:T(8,128)(2,1)} %param.15) | data formatting | bytes 4194304 | tf_op args[4]
  13.0 13.1 %all-to-all-start.1 = ((bf16[128,64,128]{0,2,1:T(8,128)(2,1)}), bf16[128,64,128]{0,2,1:T(8,128)(2,1)S(1)}, u32[]{:S(2)}, u32[]{:S(2)}) async-start(bf16[128,64,128]{0,2,1:T(8,128)(2,1)} %bitcast.14), calls=%async_computation.1 | async-start | bytes 4194304 | tf_op jit(solution)/shard_map/all_to_all | solution.py:78
  26.2 0.1 convert_reduce_fusion
  26.3 9.2 %all-reduce.1 = (f32[128]{0:T(128)S(1)}, f32[128]{0:T(128)S(1)}) all-reduce(f32[128]{0:T(128)S(1)} %get-tuple-element.63, f32[128]{0:T(128)S(1)} %get-tuple-element.62), channel_id=1, replica_groups=mesh['seq'=64,'hid'=4] {'hid'}, use_global_device_ids=true, to_apply=%region_3.0 | all-reduce | flops 256 | bytes 2048 | tf_op jit(solution)/shard_map/psum | solution.py:38
  35.5 47.9 %all-to-all-done.1 = bf16[128,64,128]{0,2,1:T(8,128)(2,1)S(1)} async-done(((bf16[128,64,128]{0,2,1:T(8,128)(2,1)}), bf16[128,64,128]{0,2,1:T(8,128)(2,1)S(1)}, u32[]{:S(2)}, u32[]{:S(2)}) %all-to-all-start.1) | async-done | bytes 2097184 | tf_op jit(solution)/shard_map/all_to_all | solution.py:78
  83.4 23.3 %all-gather.2.cloned.1.call-done = bf16[8192,512]{1,0:T(8,128)(2,1)} async-done(((bf16[128,512]{1,0:T(8,128)(2,1)}), bf16[8192,512]{1,0:T(8,128)(2,1)}) %all-gather.2.cloned.1.call-update) | async-done | bytes 8388624 | tf_op jit(solution)/shard_map/all_gather | solution.py:80
  106.7 9.3 %conditional.3 = (f32[128,512]{1,0:T(8,128)S(1)}) conditional(s32[]{:T(128)} %convert_element_type.37, () %tuple.24, (s32[]{:T(128)}, s32[1,128]{1,0:T(1,128)S(1)}, bf16[64,128,128]{1,2,0:T(8,128)(2,1)S(1)}, bf16[8192,512]{1,0:T(8,128)(2,1)}) %tuple.47), branch_computations={%region_6.0_spmd, %region_7.8_spmd} | conditional | flops 1075839104 | bytes 23332392 | solution.py:91
  106.7 1.4 copy-done
  108.1 3.2 copy.18
  111.3 4.7 %fusion.7 = f32[128,512]{1,0:T(8,128)S(1)} fusion(bf16[8192,512]{1,0:T(8,128)(2,1)} %get-tuple-element.35, bf16[8192,128]{1,0:T(8,128)(2,1)S(1)} %bitcast.12, s32[128]{0:T(128)S(1)} %add_bitcast_fusion.1), kind=kOutput, calls=%fused_computation.10 | convolution fusion | flops 1075838976 | bytes 10748416 | tf_op jit(solution)/shard_map/cond/branch_1_fun/nt,nc->tc/dot_general | solution.py:87
  116.0 0.2 fusion.25
  116.2 9.0 %all-reduce = (f32[128]{0:T(128)S(1)}, f32[128]{0:T(128)S(1)}, f32[128]{0:T(128)}) all-reduce(f32[128]{0:T(128)S(1)} %get-tuple-element.59, f32[128]{0:T(128)S(1)} %get-tuple-element.60, f32[128]{0:T(128)S(1)} %get-tuple-element.69), channel_id=1, replica_groups=mesh['seq'=64,'hid'=4] {'hid'}, use_global_device_ids=true, to_apply=%region_11.12 | all-reduce | flops 384 | bytes 3072 | tf_op jit(solution)/shard_map/psum | solution.py:101
  125.2 0.8 fusion.24
  126.1 4.2 %tile.2 = bf16[64,128,512]{2,1,0:T(8,128)(2,1)} broadcast(bf16[128,512]{1,0:T(8,128)(2,1)S(1)} %get-tuple-element.72), dimensions={1,2} | broadcast | bytes 8519680 | tf_op jit(solution)/shard_map/tile | solution.py:58
  130.3 9.2 %all-to-all-start = ((bf16[64,128,512]{2,1,0:T(8,128)(2,1)}), bf16[64,128,512]{2,1,0:T(8,128)(2,1)}, u32[]{:S(2)}, u32[]{:S(2)}) async-start(bf16[64,128,512]{2,1,0:T(8,128)(2,1)} %tile.2), calls=%async_computation | async-start | bytes 16777216 | tf_op jit(solution)/shard_map/all_to_all | solution.py:57
  139.5 0.0 reduce-scatter.2.cloned.1.call-start
  139.5 182.2 %all-to-all-done = bf16[64,128,512]{2,1,0:T(8,128)(2,1)} async-done(((bf16[64,128,512]{2,1,0:T(8,128)(2,1)}), bf16[64,128,512]{2,1,0:T(8,128)(2,1)}, u32[]{:S(2)}, u32[]{:S(2)}) %all-to-all-start) | async-done | bytes 8388640 | tf_op jit(solution)/shard_map/all_to_all | solution.py:57
  321.8 0.0 copy-done.1
  321.8 12.9 %conditional.2 = (f32[128,512]{1,0:T(8,128)S(1)}, f32[128,8192]{1,0:T(8,128)}) conditional(s32[]{:T(128)} %convert_element_type.31, () %tuple.22, (s32[]{:T(128)}, s32[128,1]{0,1:T(1,128)S(1)}, bf16[128,8192]{1,0:T(8,128)(2,1)S(1)}, bf16[64,128,512]{2,1,0:T(8,128)(2,1)}, bf16[128,512]{1,0:T(8,128)(2,1)S(1)}) %tuple.49), branch_computations={%region_4.0_spmd, %region_5.0_spmd} | conditional | flops 2151677952 | bytes 23463956 | solution.py:72
  321.8 4.7 %fusion.1 = f32[128,512]{1,0:T(8,128)S(1)} fusion(bf16[8192,512]{1,0:T(8,128)(2,1)} %bitcast.1, bf16[128,8192]{1,0:T(8,128)(2,1)S(1)} %get-tuple-element.29, s32[128]{0:T(128)S(1)} %add_bitcast_fusion), kind=kOutput, calls=%fused_computation.3 | convolution fusion | flops 1075838976 | bytes 10748416 | tf_op jit(solution)/shard_map/cond/branch_1_fun/dot_general | solution.py:67
  326.5 8.2 %convolution_select_fusion = f32[128,8192]{1,0:T(8,128)} fusion(bf16[128,512]{1,0:T(8,128)(2,1)S(1)} %get-tuple-element.31, bf16[8192,512]{1,0:T(8,128)(2,1)} %bitcast.1, s32[128]{0:T(128)S(1)} %add_bitcast_fusion), kind=kOutput, calls=%fused_computation | convolution fusion | flops 1075838976 | bytes 12714496 | tf_op jit(solution)/shard_map/cond/branch_1_fun/tc,nc->tn/dot_general | solution.py:68
  334.7 0.0 reduce-scatter.2.cloned.1.call-update
  334.7 0.1 broadcast_in_dim.8
  334.9 22.9 %all_to_all.33 = f32[64,1,1024]{2,1,0:T(1,128)S(1)} all-to-all(f32[64,1,1024]{2,1,0:T(1,128)S(1)} %broadcast_in_dim.8), channel_id=1, replica_groups=mesh['seq'=64,'hid'=4] {'seq'}, dimensions={0} | all-to-all | bytes 524288 | tf_op jit(solution)/shard_map/all_to_all | solution.py:11
  357.8 0.2 reduce_sum.78
  358.0 0.6 fusion.28
  358.6 0.8 fusion.13
  359.3 23.4 %reduce-scatter.2.cloned.1.call-done = f32[128,2048]{1,0:T(8,128)} async-done(((f32[128,8192]{1,0:T(8,128)}), f32[128,2048]{1,0:T(8,128)}) %reduce-scatter.2.cloned.1.call-update) | async-done | bytes 1048592 | tf_op jit(solution)/shard_map/reduce_scatter | solution.py:77
  (20 shorter events, 0.1 us)
Async XLA Ops:
  7.2 99.5 %all-gather.2.cloned.1.call-start = ((), (), s32[]{:S(2)}) async-start(), calls=%async_computation.4 | async-start | bytes 8519680 | tf_op jit(solution)/shard_map/all_gather | solution.py:80
  8.9 17.3 %copy-start.3 = (bf16[128,512]{1,0:T(8,128)(2,1)S(1)}, bf16[128,512]{1,0:T(8,128)(2,1)}, u32[]{:S(2)}) copy-start(bf16[128,512]{1,0:T(8,128)(2,1)} %param.12) | copy-start | bytes 393220
  13.0 70.4 %all-to-all-start.1 = ((bf16[128,64,128]{0,2,1:T(8,128)(2,1)}), bf16[128,64,128]{0,2,1:T(8,128)(2,1)S(1)}, u32[]{:S(2)}, u32[]{:S(2)}) async-start(bf16[128,64,128]{0,2,1:T(8,128)(2,1)} %bitcast.14), calls=%async_computation.1 | async-start | bytes 4194304 | tf_op jit(solution)/shard_map/all_to_all | solution.py:78
  106.7 9.3 %copy-start.5 = (f32[512]{0:T(512)S(1)}, f32[512]{0:T(512)}, u32[]{:S(2)}) copy-start(f32[512]{0:T(512)} %param.13) | copy-start | bytes 6148
  106.7 18.6 %copy-start.6 = (f32[512]{0:T(512)S(1)}, f32[512]{0:T(512)}, u32[]{:S(2)}) copy-start(f32[512]{0:T(512)} %param.14) | copy-start | bytes 6148
  106.7 1.4 copy-start
  130.3 191.5 %copy-start.1 = (bf16[128,8192]{1,0:T(8,128)(2,1)S(1)}, bf16[128,8192]{1,0:T(8,128)(2,1)}, u32[]{:S(2)}) copy-start(bf16[128,8192]{1,0:T(8,128)(2,1)} %param.15) | copy-start | bytes 6291460
  130.3 191.5 %copy-start.2 = (bf16[128,512]{1,0:T(8,128)(2,1)S(1)}, bf16[128,512]{1,0:T(8,128)(2,1)}, u32[]{:S(2)}) copy-start(bf16[128,512]{1,0:T(8,128)(2,1)} %get-tuple-element.70) | copy-start | bytes 393220
  130.3 191.5 %all-to-all-start = ((bf16[64,128,512]{2,1,0:T(8,128)(2,1)}), bf16[64,128,512]{2,1,0:T(8,128)(2,1)}, u32[]{:S(2)}, u32[]{:S(2)}) async-start(bf16[64,128,512]{2,1,0:T(8,128)(2,1)} %tile.2), calls=%async_computation | async-start | bytes 16777216 | tf_op jit(solution)/shard_map/all_to_all | solution.py:57
  139.5 243.2 %reduce-scatter.2.cloned.1.call-start = ((), (), s32[]{:S(2)}) async-start(), calls=%async_computation.5 | async-start | bytes 5242880 | tf_op jit(solution)/shard_map/reduce_scatter | solution.py:77
  334.7 23.9 %copy-start.4 = (bf16[128,512]{1,0:T(8,128)(2,1)S(1)}, bf16[128,512]{1,0:T(8,128)(2,1)}, u32[]{:S(2)}) copy-start(bf16[128,512]{1,0:T(8,128)(2,1)} %param.17) | copy-start | bytes 393220
  334.7 23.9 %copy-start.7 = (f32[128]{0:T(128)S(1)}, f32[128]{0:T(128)}, u32[]{:S(2)}) copy-start(f32[128]{0:T(128)} %param.16) | copy-start | bytes 1540
Sparse Core Ops, SparseCore 0:
  11.3 95.3 all-gather.1
  334.8 47.8 reduce-scatter.1
